TPU v7x, 8 devices: a whole 2x2x1 slice. The times are simulated.
8 devices in a mesh: replica: 1 (over z), data2: 2 (over y), data: 4 (over x, core).
Axes of the slice: x: 2, y: 2, z: 1, core: 2. Of those that a mesh axis runs over, the one named last changes fastest.
Arguments:
- q_hidden: bfloat16 [16, 32, 768], P(('replica', 'data2', 'data'))
- d_hidden: bfloat16 [16, 8192, 768], P(('replica', 'data2', 'data'))
- w_proj: bfloat16 [768, 128], replicated
- q_mask: int32 [16, 32], P(('replica', 'data2', 'data'))
- d_mask: int32 [16, 8192], P(('replica', 'data2', 'data'))
- temperature: float32 [], replicated
Outputs:
- output 1: float32 [16], P(('replica', 'data2', 'data'))
- output 2: float32 [1], P('replica')
All inputs are finite; a program needn't handle non-finite values.
Results may differ from a plain program's by a relative error of at most 0.00163984.
Values are sent between devices in bfloat16 or wider.
A program may use at most 1 GiB of HBM per device.

v0:
```python
import jax
import jax.numpy as jnp
from jax import lax
from jax.sharding import PartitionSpec as P

NORM_EPS = 1e-6
GROUP_AXES = ('data2', 'data')
ROW_AXES = ('replica', 'data2', 'data')


def project(hidden, w_proj):
    proj_f32 = jnp.einsum('bld,de->ble', hidden, w_proj, preferred_element_type=jnp.float32)
    row_norm = jnp.sqrt(jnp.sum(proj_f32 * proj_f32, axis=-1, keepdims=True) + NORM_EPS)
    return (proj_f32 / row_norm).astype(jnp.bfloat16)


def block_scores(q_block, d_tok, d_valid):
    sim_vals = jnp.einsum('qtd,psd->qtps', q_block, d_tok, preferred_element_type=jnp.float32)
    sim_vals = jnp.where(d_valid[None, None], sim_vals, -jnp.inf)
    return jnp.sum(jnp.max(sim_vals, axis=-1), axis=1)


def row_losses(row_scores, value_a11, my_index, per_dev):
    logits = row_scores / value_a11
    row_max = jnp.max(logits, axis=1, keepdims=True)
    log_norm = row_max[:, 0] + jnp.log(jnp.sum(jnp.exp(logits - row_max), axis=1))
    pos_tile = lax.dynamic_slice_in_dim(logits, my_index * per_dev, per_dev, axis=1)
    return log_norm - jnp.diagonal(pos_tile)


def solution(mesh):
    outer_size = mesh.shape['data2']
    inner_size = mesh.shape['data']
    group_size = outer_size * inner_size

    def device_fn(q_hidden, d_hidden, w_proj, q_mask, d_mask, value_a11):
        per_dev, q_len = q_mask.shape
        proj_dim = w_proj.shape[1]
        q_tok = jnp.where(q_mask[:, :, None] > 0, project(q_hidden, w_proj), jnp.zeros((), jnp.bfloat16))
        d_tok = project(d_hidden, w_proj)
        d_valid = d_mask > 0
        all_q = lax.all_gather(q_tok, GROUP_AXES, axis=0, tiled=True)
        all_q = all_q.reshape(group_size, per_dev, q_len, proj_dim)

        def score_block(q_block):
            return block_scores(q_block, d_tok, d_valid)

        col_scores = lax.map(score_block, all_q).reshape(outer_size, inner_size, per_dev, per_dev)
        col_scores = lax.all_to_all(col_scores, 'data', 1, 1, tiled=True)
        col_scores = lax.all_to_all(col_scores, 'data2', 0, 0, tiled=True)
        row_scores = jnp.transpose(col_scores, (2, 0, 1, 3)).reshape(per_dev, group_size * per_dev)
        my_index = lax.axis_index('data2') * inner_size + lax.axis_index('data')
        loss_rows = row_losses(row_scores, value_a11, my_index, per_dev)
        loss_mean = lax.psum(jnp.sum(loss_rows), GROUP_AXES) / (group_size * per_dev)
        return loss_rows, loss_mean.reshape(1)

    return jax.shard_map(
        device_fn,
        mesh=mesh,
        in_specs=(P(ROW_AXES), P(ROW_AXES), P(), P(ROW_AXES), P(ROW_AXES), P()),
        out_specs=(P(ROW_AXES), P('replica')),
        check_vma=False,
    )
```

profile of v0, /device:TPU:0, one launch (start us, length us, event | category | flops | bytes accessed | tf_op | source)
XLA Modules:
  0.0 116.7 jit_solution(1582524534863845201)
XLA Ops:
  0.6 0.0 copy-start
  0.7 0.9 copy-done
  1.6 15.0 %multiply_reduce_fusion = (f32[2,8192]{1,0:T(2,128)S(1)}, f32[2,8192,128]{1,2,0:T(8,128)}) fusion(bf16[2,8192,768]{2,1,0:T(8,128)(2,1)} %param.9, bf16[768,128]{1,0:T(8,128)(2,1)S(1)} %copy-done), kind=kOutput, calls=%fused_computation.9 | convolution fusion | flops 3225403392 | bytes 33816576 | tf_op jit(solution)/shard_map/bld,de->ble/dot_general | solution.py:12
  16.6 0.1 add_sqrt_fusion
  16.7 0.0 copy-start.1
  16.7 0.0 copy-start.3
  16.7 0.0 copy-start.2
  16.7 6.2 %divide_convert_fusion = bf16[2,8192,128]{1,2,0:T(8,128)(2,1)} fusion(f32[2,8192,128]{1,2,0:T(8,128)} %get-tuple-element.62, f32[2,8192]{1,0:T(2,128)S(1)} %add_sqrt_fusion), kind=kLoop, calls=%fused_computation.8 | loop fusion | flops 4194304 | bytes 12648448 | tf_op jit(solution)/shard_map/convert_element_type | solution.py:14
  22.8 6.4 %copy.17 = bf16[2,8192,128]{2,1,0:T(8,128)(2,1)} copy(bf16[2,8192,128]{1,2,0:T(8,128)(2,1)} %divide_convert_fusion) | data formatting | bytes 8388608 | tf_op jit(solution)/shard_map/while | solution.py:48
  29.2 0.0 copy-done.1
  29.2 0.2 multiply_reduce_fusion.1
  29.5 0.0 copy-done.3
  29.5 0.1 fusion.11
  29.6 13.9 %all_gather.3 = bf16[16,32,128]{2,1,0:T(8,128)(2,1)S(1)} all-gather(bf16[2,32,128]{2,1,0:T(8,128)(2,1)S(1)} %fusion.11), channel_id=1, replica_groups=mesh['replica'=1,'data2'=2,'data'=4] {'data2','data'}, dimensions={0}, use_global_device_ids=true | all-gather | bytes 147456 | tf_op jit(solution)/shard_map/all_gather | solution.py:42
  43.5 0.0 copy-done.2
  43.6 31.6 %while.10 = (s32[]{:T(128)}, f32[8,2,2]{2,1,0:T(2,128)S(1)}, pred[2,8192]{1,0:T(4,128)(4,1)S(1)}, bf16[8,2,32,128]{3,2,1,0:T(8,128)(2,1)S(1)}, bf16[2,8192,128]{2,1,0:T(8,128)(2,1)}, /*index=5*/s32[]{:T(128)}, f32[]{:T(128)}) while((s32[]{:T(128)}, f32[8,2,2]{2,1,0:T(2,128)S(1)}, pred[2,8192]{1,0:T(4,128)(4,1)S(1)}, ...), condition=%wide.region_5.6_spmd, body=%wide.region_2.5_spmd.sunk | while | flops 270532608 | bytes 4246633 | solution.py:48
  43.6 3.8 %fusion.21 = f32[2,32,2]{1,2,0:T(2,128)S(1)} fusion(bf16[2,8192,128]{2,1,0:T(8,128)(2,1)} %get-tuple-element.112, pred[2,8192]{1,0:T(4,128)(4,1)S(1)} %get-tuple-element.110, bf16[8,2,32,128]{3,2,1,0:T(8,128)(2,1)S(1)} %get-tuple-element.111, s32[]{:T(128)} %get-tuple-element.101), kind=kOutput, calls=%fused_computation.3.clone.1 | convolution fusion | flops 270532480 | bytes 4243972 | tf_op jit(solution)/shard_map/while/body/eval_jaxpr/qtd,psd->qtps/dot_general | solution.py:18
  47.4 0.1 reduce_sum.54
  47.5 3.8 %fusion.21 = f32[2,32,2]{1,2,0:T(2,128)S(1)} fusion(bf16[2,8192,128]{2,1,0:T(8,128)(2,1)} %get-tuple-element.112, pred[2,8192]{1,0:T(4,128)(4,1)S(1)} %get-tuple-element.110, bf16[8,2,32,128]{3,2,1,0:T(8,128)(2,1)S(1)} %get-tuple-element.111, s32[]{:T(128)} %get-tuple-element.101), kind=kOutput, calls=%fused_computation.3.clone.1 | convolution fusion | flops 270532480 | bytes 4243972 | tf_op jit(solution)/shard_map/while/body/eval_jaxpr/qtd,psd->qtps/dot_general | solution.py:18
  51.4 0.1 reduce_sum.54
  51.5 3.8 %fusion.21 = f32[2,32,2]{1,2,0:T(2,128)S(1)} fusion(bf16[2,8192,128]{2,1,0:T(8,128)(2,1)} %get-tuple-element.112, pred[2,8192]{1,0:T(4,128)(4,1)S(1)} %get-tuple-element.110, bf16[8,2,32,128]{3,2,1,0:T(8,128)(2,1)S(1)} %get-tuple-element.111, s32[]{:T(128)} %get-tuple-element.101), kind=kOutput, calls=%fused_computation.3.clone.1 | convolution fusion | flops 270532480 | bytes 4243972 | tf_op jit(solution)/shard_map/while/body/eval_jaxpr/qtd,psd->qtps/dot_general | solution.py:18
  55.3 0.1 reduce_sum.54
  55.4 3.8 %fusion.21 = f32[2,32,2]{1,2,0:T(2,128)S(1)} fusion(bf16[2,8192,128]{2,1,0:T(8,128)(2,1)} %get-tuple-element.112, pred[2,8192]{1,0:T(4,128)(4,1)S(1)} %get-tuple-element.110, bf16[8,2,32,128]{3,2,1,0:T(8,128)(2,1)S(1)} %get-tuple-element.111, s32[]{:T(128)} %get-tuple-element.101), kind=kOutput, calls=%fused_computation.3.clone.1 | convolution fusion | flops 270532480 | bytes 4243972 | tf_op jit(solution)/shard_map/while/body/eval_jaxpr/qtd,psd->qtps/dot_general | solution.py:18
  59.3 0.1 reduce_sum.54
  59.4 3.8 %fusion.21 = f32[2,32,2]{1,2,0:T(2,128)S(1)} fusion(bf16[2,8192,128]{2,1,0:T(8,128)(2,1)} %get-tuple-element.112, pred[2,8192]{1,0:T(4,128)(4,1)S(1)} %get-tuple-element.110, bf16[8,2,32,128]{3,2,1,0:T(8,128)(2,1)S(1)} %get-tuple-element.111, s32[]{:T(128)} %get-tuple-element.101), kind=kOutput, calls=%fused_computation.3.clone.1 | convolution fusion | flops 270532480 | bytes 4243972 | tf_op jit(solution)/shard_map/while/body/eval_jaxpr/qtd,psd->qtps/dot_general | solution.py:18
  63.2 0.1 reduce_sum.54
  63.3 3.8 %fusion.21 = f32[2,32,2]{1,2,0:T(2,128)S(1)} fusion(bf16[2,8192,128]{2,1,0:T(8,128)(2,1)} %get-tuple-element.112, pred[2,8192]{1,0:T(4,128)(4,1)S(1)} %get-tuple-element.110, bf16[8,2,32,128]{3,2,1,0:T(8,128)(2,1)S(1)} %get-tuple-element.111, s32[]{:T(128)} %get-tuple-element.101), kind=kOutput, calls=%fused_computation.3.clone.1 | convolution fusion | flops 270532480 | bytes 4243972 | tf_op jit(solution)/shard_map/while/body/eval_jaxpr/qtd,psd->qtps/dot_general | solution.py:18
  67.2 0.1 reduce_sum.54
  67.3 3.8 %fusion.21 = f32[2,32,2]{1,2,0:T(2,128)S(1)} fusion(bf16[2,8192,128]{2,1,0:T(8,128)(2,1)} %get-tuple-element.112, pred[2,8192]{1,0:T(4,128)(4,1)S(1)} %get-tuple-element.110, bf16[8,2,32,128]{3,2,1,0:T(8,128)(2,1)S(1)} %get-tuple-element.111, s32[]{:T(128)} %get-tuple-element.101), kind=kOutput, calls=%fused_computation.3.clone.1 | convolution fusion | flops 270532480 | bytes 4243972 | tf_op jit(solution)/shard_map/while/body/eval_jaxpr/qtd,psd->qtps/dot_general | solution.py:18
  71.1 0.1 reduce_sum.54
  71.2 3.8 %fusion.21 = f32[2,32,2]{1,2,0:T(2,128)S(1)} fusion(bf16[2,8192,128]{2,1,0:T(8,128)(2,1)} %get-tuple-element.112, pred[2,8192]{1,0:T(4,128)(4,1)S(1)} %get-tuple-element.110, bf16[8,2,32,128]{3,2,1,0:T(8,128)(2,1)S(1)} %get-tuple-element.111, s32[]{:T(128)} %get-tuple-element.101), kind=kOutput, calls=%fused_computation.3.clone.1 | convolution fusion | flops 270532480 | bytes 4243972 | tf_op jit(solution)/shard_map/while/body/eval_jaxpr/qtd,psd->qtps/dot_general | solution.py:18
  75.1 0.1 reduce_sum.54
  75.2 0.7 copy.19
  75.9 3.2 %all-to-all-start = ((f32[2,4,2,2]{0,3,2,1:T(2,128)}), f32[2,4,2,2]{0,3,2,1:T(2,128)S(1)}, u32[]{:S(2)}, u32[]{:S(2)}) async-start(f32[2,4,2,2]{0,3,2,1:T(2,128)} %copy.19), calls=%async_computation | async-start | bytes 16384 | tf_op jit(solution)/shard_map/all_to_all | solution.py:49
  79.8 2.9 %all-to-all-done = f32[2,4,2,2]{0,3,2,1:T(2,128)S(1)} async-done(((f32[2,4,2,2]{0,3,2,1:T(2,128)}), f32[2,4,2,2]{0,3,2,1:T(2,128)S(1)}, u32[]{:S(2)}, u32[]{:S(2)}) %all-to-all-start) | async-done | bytes 160 | tf_op jit(solution)/shard_map/all_to_all | solution.py:49
  82.7 0.7 copy.20
  83.4 3.2 %all-to-all-start.1 = ((f32[2,4,2,2]{1,3,2,0:T(2,128)}), f32[2,4,2,2]{1,3,2,0:T(2,128)S(1)}, u32[]{:S(2)}, u32[]{:S(2)}) async-start(f32[2,4,2,2]{1,3,2,0:T(2,128)} %copy.20), calls=%async_computation.1 | async-start | bytes 8192 | tf_op jit(solution)/shard_map/all_to_all | solution.py:50
  86.7 3.6 %all-to-all-done.1 = f32[2,4,2,2]{1,3,2,0:T(2,128)S(1)} async-done(((f32[2,4,2,2]{1,3,2,0:T(2,128)}), f32[2,4,2,2]{1,3,2,0:T(2,128)S(1)}, u32[]{:S(2)}, u32[]{:S(2)}) %all-to-all-start.1) | async-done | bytes 160 | tf_op jit(solution)/shard_map/all_to_all | solution.py:50
  90.2 0.1 fusion.13
  90.3 0.1 copy.21
  90.4 0.1 div.41
  90.5 0.2 exponential_reduce_fusion
  90.7 0.1 constant_dynamic-slice_fusion
  90.8 0.6 gather_fusion
  91.4 1.1 fusion.12
  92.5 22.4 %psum.7 = f32[]{:T(128)} all-reduce(f32[]{:T(128)} %get-tuple-element.55), channel_id=1, replica_groups=mesh['replica'=1,'data2'=2,'data'=4] {'data2','data'}, use_global_device_ids=true, to_apply=%region_9.10 | all-reduce | flops 1 | bytes 8 | tf_op jit(solution)/shard_map/psum | solution.py:54
  (13 shorter events, 0.2 us)
Async XLA Ops:
  0.6 0.9 copy-start
  16.7 12.6 %copy-start.1 = (bf16[2,32,768]{2,1,0:T(8,128)(2,1)S(1)}, bf16[2,32,768]{2,1,0:T(8,128)(2,1)}, u32[]{:S(2)}) copy-start(bf16[2,32,768]{2,1,0:T(8,128)(2,1)} %param.8) | copy-start | bytes 294916
  16.7 12.8 %copy-start.3 = (s32[2,32]{1,0:T(2,128)S(1)}, s32[2,32]{1,0:T(2,128)}, u32[]{:S(2)}) copy-start(s32[2,32]{1,0:T(2,128)} %param.11) | copy-start | bytes 772
  16.7 26.8 %copy-start.2 = (s32[2,8192]{1,0:T(2,128)S(1)}, s32[2,8192]{1,0:T(2,128)}, u32[]{:S(2)}) copy-start(s32[2,8192]{1,0:T(2,128)} %param.12) | copy-start | bytes 196612
  75.9 6.8 %all-to-all-start = ((f32[2,4,2,2]{0,3,2,1:T(2,128)}), f32[2,4,2,2]{0,3,2,1:T(2,128)S(1)}, u32[]{:S(2)}, u32[]{:S(2)}) async-start(f32[2,4,2,2]{0,3,2,1:T(2,128)} %copy.19), calls=%async_computation | async-start | bytes 16384 | tf_op jit(solution)/shard_map/all_to_all | solution.py:49
  83.4 6.8 %all-to-all-start.1 = ((f32[2,4,2,2]{1,3,2,0:T(2,128)}), f32[2,4,2,2]{1,3,2,0:T(2,128)S(1)}, u32[]{:S(2)}, u32[]{:S(2)}) async-start(f32[2,4,2,2]{1,3,2,0:T(2,128)} %copy.20), calls=%async_computation.1 | async-start | bytes 8192 | tf_op jit(solution)/shard_map/all_to_all | solution.py:50
where the time goes:
time: 118 us; the launch traced here: 117 us
  matrix products  46 us (39%)
  blocking collectives  36.4 us (31%)
  local copies, waits for them, and re-layouts  9.74 us (8%)
  other arithmetic  8.49 us (7%)
  starting transfers between devices  6.47 us (5%)
  waiting for transfers between devices  6.46 us (5%)
  between operations  3.19 us (3%)
    dot_general x8, matrix products, block_scores(): jnp.einsum('qtd,psd->qtps', q_block, d_tok, preferred_element_type=jnp.fl...  30.8 us
    psum x1, blocking collectives, device_fn(): lax.psum(jnp.sum(loss_rows), GROUP_AXES) / (group_size * per_dev)  22.4 us
    dot_general x2, matrix products, project(): jnp.einsum('bld,de->ble', hidden, w_proj, preferred_element_type=jnp.floa...  15.3 us
    all_gather x1, blocking collectives, device_fn(): all_q = lax.all_gather(q_tok, GROUP_AXES, axis=0, tiled=True)  13.9 us
    while x1, local copies, waits for them, and re-layouts, device_fn(): lax.map(score_block, all_q)  6.36 us
    convert_element_type x1, other arithmetic, project(): return (proj_f32 / row_norm).astype(jnp.bfloat16)  6.16 us
    all_to_all x1, waiting for transfers between devices, device_fn(): col_scores = lax.all_to_all(col_scores, 'data2', 0, 0, tiled=True)  3.57 us
    all_to_all x1, starting transfers between devices, device_fn(): col_scores = lax.all_to_all(col_scores, 'data', 1, 1, tiled=True)  3.25 us
  transfers between devices with their start and end apart: 2, of which 2 were waited for; matrix products, arithmetic and copies ran while one was open for 0% of the time, Pallas kernels for 0%

commit v1 on v0

v1 whole, which is shorter than its diff:
```python
import functools

import jax
import jax.numpy as jnp
from jax import lax
from jax.experimental import pallas as pl
from jax.experimental.pallas import tpu as pltpu
from jax.sharding import PartitionSpec as P

NORM_EPS = 1e-6
ROW_AXES = ('replica', 'data2', 'data')
BLOCK = 1024
LAG = 8
NEG = float('-inf')


def kernel(sizes, q_hbm, d_hbm, w_hbm, qm_ref, dm_ref, temp_ref, rows_ref, mean_ref,
           h_ref, q_ref, w_ref, wt_ref, et_ref, qall_ref, best_ref, sall_ref,
           in_sem, h_sem, q_send, q_recv, s_send, s_recv):
    outer, inner, per_dev, q_len, d_len, hidden, proj = sizes
    group = outer * inner
    n_blocks = per_dev * d_len // BLOCK
    doc_blocks = d_len // BLOCK
    d2 = lax.axis_index('data2')
    d1 = lax.axis_index('data')
    me = d2 * inner + d1

    def peer(step):
        other = lax.rem(me + step, group)
        return other, {'data2': other // inner, 'data': lax.rem(other, inner)}

    w_copy = pltpu.make_async_copy(w_hbm, w_ref, in_sem.at[0])
    q_copy = pltpu.make_async_copy(q_hbm, q_ref, in_sem.at[1])
    w_copy.start()
    q_copy.start()

    def h_copy(block):
        return pltpu.make_async_copy(
            d_hbm.at[pl.ds(block * BLOCK, BLOCK)], h_ref.at[pl.ds(block * BLOCK, BLOCK)], h_sem.at[block])

    for block in range(n_blocks):
        h_copy(block).start()

    barrier = pltpu.get_barrier_semaphore()
    for step in range(1, group):
        pl.semaphore_signal(barrier, inc=1, device_id=peer(step)[1], device_id_type=pl.DeviceIdType.MESH)

    w_copy.wait()
    q_copy.wait()
    y = jnp.dot(q_ref[...], w_ref[...], preferred_element_type=jnp.float32)
    unit = y * lax.rsqrt(jnp.sum(y * y, axis=1, keepdims=True) + NORM_EPS)
    eye = lax.broadcasted_iota(jnp.int32, (q_len, q_len), 0) == lax.broadcasted_iota(jnp.int32, (q_len, q_len), 1)
    for i in range(per_dev):
        keep = jnp.sum(jnp.where(eye, qm_ref[pl.ds(i, 1), :], 0), axis=1, keepdims=True)
        rows = jnp.where(keep > 0, unit[i * q_len:(i + 1) * q_len], 0.0)
        qall_ref[me, pl.ds(i * q_len, q_len), :] = rows.astype(jnp.bfloat16)
    wt_ref[...] = jnp.transpose(w_ref[...], (1, 0))

    pl.semaphore_wait(barrier, group - 1)

    def q_copy_to(step):
        return pltpu.make_async_remote_copy(
            src_ref=qall_ref.at[me], dst_ref=qall_ref.at[me], send_sem=q_send.at[step], recv_sem=q_recv.at[me],
            device_id=peer(step)[1], device_id_type=pl.DeviceIdType.MESH)

    for step in range(1, group):
        q_copy_to(step).start()

    best_ref[...] = jnp.full(best_ref.shape, NEG, jnp.float32)

    def project(block):
        h_copy(block).wait()
        h = h_ref[pl.ds(block * BLOCK, BLOCK), :]
        y = lax.dot_general(wt_ref[...], h, (((1,), (1,)), ((), ())), preferred_element_type=jnp.float32)
        inv = lax.rsqrt(jnp.sum(y * y, axis=0, keepdims=True) + NORM_EPS)
        et_ref[block] = (y * inv).astype(jnp.bfloat16)

    def score(block):
        doc = block // doc_blocks
        col = lax.rem(block, doc_blocks) * BLOCK
        q = qall_ref[...].reshape(group * per_dev * q_len, proj)
        for t in range(0, BLOCK, 512):
            s = jnp.dot(q, et_ref[block, :, t:t + 512], preferred_element_type=jnp.float32)
            valid = dm_ref[pl.ds(doc, 1), pl.ds(pl.multiple_of(col + t, 128), 512)] > 0
            s = s + jnp.where(valid, 0.0, NEG)
            m = jnp.maximum(jnp.maximum(s[:, :128], s[:, 128:256]), jnp.maximum(s[:, 256:384], s[:, 384:]))
            best_ref[doc] = jnp.maximum(best_ref[doc], m)

    def loop(lo, hi, body):
        def step(i, carry):
            body(i)
            return carry
        lax.fori_loop(lo, hi, step, 0)

    loop(0, LAG, project)

    for step in range(1, group):
        other = lax.rem(me + step, group)
        pltpu.make_async_remote_copy(
            src_ref=qall_ref.at[other], dst_ref=qall_ref.at[other], send_sem=q_send.at[step],
            recv_sem=q_recv.at[other], device_id=peer(step)[1], device_id_type=pl.DeviceIdType.MESH).wait_recv()

    def both(block):
        project(block)
        score(block - LAG)

    loop(LAG, n_blocks, both)
    loop(n_blocks - LAG, n_blocks, score)

    n_rows = group * per_dev
    lane = lax.broadcasted_iota(jnp.int32, (n_rows, 128), 1)
    mine = jnp.zeros((n_rows, 128), jnp.float32)
    for d in range(per_dev):
        m = jnp.max(best_ref[d], axis=1, keepdims=True)
        m = jnp.broadcast_to(m, (n_rows * q_len, 128)).reshape(n_rows, q_len, 128)
        mine = jnp.where(lane == me * per_dev + d, jnp.sum(m, axis=1), mine)
    sall_ref[me] = mine

    def s_copy_to(step):
        return pltpu.make_async_remote_copy(
            src_ref=sall_ref.at[me], dst_ref=sall_ref.at[me], send_sem=s_send.at[step], recv_sem=s_recv.at[me],
            device_id=peer(step)[1], device_id_type=pl.DeviceIdType.MESH)

    for step in range(1, group):
        s_copy_to(step).start()
    for step in range(1, group):
        q_copy_to(step).wait_send()
    for step in range(1, group):
        other = lax.rem(me + step, group)
        pltpu.make_async_remote_copy(
            src_ref=sall_ref.at[other], dst_ref=sall_ref.at[other], send_sem=s_send.at[step],
            recv_sem=s_recv.at[other], device_id=peer(step)[1], device_id_type=pl.DeviceIdType.MESH).wait_recv()

    total = sall_ref[0]
    for d in range(1, group):
        total = total + sall_ref[d]
    logits = total / temp_ref[0]
    logits = jnp.where(lane < n_rows, logits, NEG)
    top = jnp.max(logits, axis=1, keepdims=True)
    log_norm = top + jnp.log(jnp.sum(jnp.exp(logits - top), axis=1, keepdims=True))
    row = lax.broadcasted_iota(jnp.int32, (n_rows, 128), 0)
    own = jnp.sum(jnp.where(row == lane, logits, 0.0), axis=1, keepdims=True)
    loss = jnp.broadcast_to(log_norm - own, (n_rows, 128))
    mean_ref[...] = jnp.sum(loss, axis=0, keepdims=True)[:, :1] / n_rows
    picked = jnp.sum(jnp.where(row == lane + me * per_dev, loss, 0.0), axis=0, keepdims=True)
    rows_ref[...] = picked[:, :per_dev]
    for step in range(1, group):
        s_copy_to(step).wait_send()


def solution(mesh):
    outer = mesh.shape['data2']
    inner = mesh.shape['data']
    group = outer * inner

    def device_fn(q_hidden, d_hidden, w_proj, q_mask, d_mask, value_a11):
        per_dev, q_len, hidden = q_hidden.shape
        d_len = d_hidden.shape[1]
        proj = w_proj.shape[1]
        sizes = (outer, inner, per_dev, q_len, d_len, hidden, proj)
        n_tok = per_dev * d_len
        n_blocks = n_tok // BLOCK
        n_rows = group * per_dev
        any_spec = pl.BlockSpec(memory_space=pl.ANY)
        vmem_spec = pl.BlockSpec(memory_space=pltpu.VMEM)
        rows, mean = pl.pallas_call(
            functools.partial(kernel, sizes),
            out_shape=(jax.ShapeDtypeStruct((1, per_dev), jnp.float32), jax.ShapeDtypeStruct((1, 1), jnp.float32)),
            in_specs=[any_spec, any_spec, any_spec, vmem_spec, vmem_spec, pl.BlockSpec(memory_space=pltpu.SMEM)],
            out_specs=(vmem_spec, vmem_spec),
            scratch_shapes=[
                pltpu.VMEM((n_tok, hidden), jnp.bfloat16),
                pltpu.VMEM((per_dev * q_len, hidden), jnp.bfloat16),
                pltpu.VMEM((hidden, proj), jnp.bfloat16),
                pltpu.VMEM((proj, hidden), jnp.bfloat16),
                pltpu.VMEM((n_blocks, proj, BLOCK), jnp.bfloat16),
                pltpu.VMEM((group, per_dev * q_len, proj), jnp.bfloat16),
                pltpu.VMEM((per_dev, n_rows * q_len, 128), jnp.float32),
                pltpu.VMEM((group, n_rows, 128), jnp.float32),
                pltpu.SemaphoreType.DMA((2,)),
                pltpu.SemaphoreType.DMA((n_blocks,)),
                pltpu.SemaphoreType.DMA((group,)),
                pltpu.SemaphoreType.DMA((group,)),
                pltpu.SemaphoreType.DMA((group,)),
                pltpu.SemaphoreType.DMA((group,)),
            ],
            compiler_params=pltpu.CompilerParams(
                collective_id=0, has_side_effects=True, vmem_limit_bytes=60 * 1024 * 1024),
            name='colbert_loss',
        )(q_hidden.reshape(per_dev * q_len, hidden), d_hidden.reshape(n_tok, hidden), w_proj, q_mask, d_mask,
          value_a11.reshape(1))
        return rows.reshape(per_dev), mean.reshape(1)

    return jax.shard_map(
        device_fn,
        mesh=mesh,
        in_specs=(P(ROW_AXES), P(ROW_AXES), P(), P(ROW_AXES), P(ROW_AXES), P()),
        out_specs=(P(ROW_AXES), P('replica')),
        check_vma=False,
    )
```

time: 118 us -> 38.3 us (0.32)
  matrix products: 46 us -> 0 us
  blocking collectives: 36.4 us -> 0 us
  Pallas kernels: 0 us -> 33.9 us
  local copies, waits for them, and re-layouts: 9.74 us -> 1.11 us
  other arithmetic: 8.49 us -> 0 us
  starting transfers between devices: 6.47 us -> 0 us
  waiting for transfers between devices: 6.46 us -> 0 us
    dot_general x10 -> x0, matrix products: 46 us -> none  [the longest x8 30.8 us: block_scores(): jnp.einsum('qtd,psd->qtps', q_block, d_tok, preferred_element_type=jnp.fl...]
    pallas_call x0 -> x1, Pallas kernels: none -> 33.9 us  [device_fn(): pl.pallas_call(functools.partial(kernel, sizes), out_shape=(jax.ShapeDtyp...]
    psum x1 -> x0, blocking collectives: 22.4 us -> none  [device_fn(): lax.psum(jnp.sum(loss_rows), GROUP_AXES) / (group_size * per_dev)]
    all_gather x1 -> x0, blocking collectives: 13.9 us -> none  [device_fn(): all_q = lax.all_gather(q_tok, GROUP_AXES, axis=0, tiled=True)]
    all_to_all x2 -> x0, starting transfers between devices: 6.47 us -> none  [the longest x1 3.25 us: device_fn(): col_scores = lax.all_to_all(col_scores, 'data', 1, 1, tiled=True)]
    all_to_all x2 -> x0, waiting for transfers between devices: 6.46 us -> none  [the longest x1 3.57 us: device_fn(): col_scores = lax.all_to_all(col_scores, 'data2', 0, 0, tiled=True)]
    while x1 -> x0, local copies, waits for them, and re-layouts: 6.36 us -> none  [device_fn(): lax.map(score_block, all_q)]
    convert_element_type x1 -> x0, other arithmetic: 6.16 us -> none  [project(): return (proj_f32 / row_norm).astype(jnp.bfloat16)]
  transfers between devices with their start and end apart: 2 -> 0, of which waited for: 2 -> 0; matrix products, arithmetic and copies ran while one was open for 0% -> 0% of each run, Pallas kernels for 0% -> 0%
where the time goes in v1:
time: 38.3 us; the launch traced here: 38.1 us
  Pallas kernels  33.9 us (89%)
  between operations  3.05 us (8%)
  local copies, waits for them, and re-layouts  1.11 us (3%)
    pallas_call x1, Pallas kernels, device_fn(): pl.pallas_call(functools.partial(kernel, sizes), out_shape=(jax.ShapeDtyp...  33.9 us
    unnamed x1, local copies, waits for them, and re-layouts  1.11 us

profile of v1, /device:TPU:0, one launch (start us, length us, event | category | flops | bytes accessed | tf_op | source)
XLA Modules:
  0.0 38.1 jit_solution(10754863554029535579)
XLA Ops:
  1.3 33.9 %colbert_loss.1 = (f32[1,2]{1,0:T(1,128)}, f32[1,1]{1,0:T(1,128)}) custom-call(bf16[64,768]{1,0:T(8,128)(2,1)} %bitcast.7, bf16[16384,768]{1,0:T(8,128)(2,1)} %bitcast.6, bf16[768,128]{1,0:T(8,128)(2,1)} %w_hbm.1, s32[2,32]{1,0:T(2,128)} %qm_ref.1, s32[2,8192]{1,0:T(2,128)} %dm_ref.1, f32[1]{0:T(128)} %bitcast.5.temp_ref), custom_call_target="tpu_custom_call" | custom-call | tf_op jit(solution)/shard_map/colbert_loss/pallas_call | solution.py:166
  35.2 1.1 %copy.11 = f32[2]{0:T(128)} copy(f32[2]{0:T(128)} %bitcast.8) | data formatting | bytes 16

commit v2 on v1

v2 whole, which is shorter than its diff:
```python
import functools

import jax
import jax.numpy as jnp
from jax import lax
from jax.experimental import pallas as pl
from jax.experimental.pallas import tpu as pltpu
from jax.sharding import PartitionSpec as P

NORM_EPS = 1e-6
ROW_AXES = ('replica', 'data2', 'data')
TILE = 256
STEP = 2 * TILE
CHUNK = 1024
LAG = 12
PIECE = 128
MASKED = -1e30
MESH = pl.DeviceIdType.MESH


def kernel(sizes, q_hbm, d_hbm, w_hbm, qm_hbm, dm_hbm, temp_hbm, rows_ref, mean_ref,
           h_ref, q_ref, w_ref, wt_ref, qm_ref, dm_ref, temp_ref, et_ref, qall_ref, best_ref, part_ref, sall_ref,
           in_sem, h_sem, q_send, q_recv, s_send, s_recv):
    outer, inner, per_dev, q_len, d_len, hidden, proj = sizes
    group = outer * inner
    n_rows = group * per_dev
    n_tok = per_dev * d_len
    n_chunks = n_tok // CHUNK
    n_steps = n_tok // STEP
    doc_steps = d_len // STEP
    k_tiles = hidden // TILE
    pieces = n_rows * q_len // PIECE
    q_rows = per_dev * q_len
    d2 = lax.axis_index('data2')
    d1 = lax.axis_index('data')
    me = d2 * inner + d1

    def peer(step):
        other = lax.rem(me + step, group)
        return other, {'data2': other // inner, 'data': lax.rem(other, inner)}

    small = [pltpu.make_async_copy(src, dst, in_sem.at[i]) for i, (src, dst) in enumerate((
        (w_hbm, w_ref), (q_hbm, q_ref), (qm_hbm, qm_ref), (dm_hbm, dm_ref), (temp_hbm, temp_ref)))]
    for copy in small:
        copy.start()

    barrier = pltpu.get_barrier_semaphore()
    for step in range(1, group):
        pl.semaphore_signal(barrier, inc=1, device_id=peer(step)[1], device_id_type=MESH)

    def h_copy(chunk):
        rows = pl.ds(chunk * CHUNK, CHUNK)
        return pltpu.make_async_copy(d_hbm.at[rows], h_ref.at[rows], h_sem.at[chunk])

    for chunk in range(n_chunks):
        h_copy(chunk).start(priority=1)

    for copy in small[:3]:
        copy.wait()

    def project_queries():
        y = jnp.dot(q_ref[...], w_ref[...], preferred_element_type=jnp.float32)
        unit = y * lax.rsqrt(jnp.sum(y * y, axis=1, keepdims=True) + NORM_EPS)
        eye = (lax.broadcasted_iota(jnp.int32, (q_len, q_len), 0)
               == lax.broadcasted_iota(jnp.int32, (q_len, q_len), 1))
        for i in range(per_dev):
            keep = jnp.sum(jnp.where(eye, qm_ref[i:i + 1, :], 0), axis=1, keepdims=True)
            rows = jnp.where(keep > 0, unit[i * q_len:(i + 1) * q_len], 0.0)
            qall_ref[me, pl.ds(i * q_len, q_len), :] = rows.astype(jnp.bfloat16)

    project_queries()
    wt_ref[...] = jnp.transpose(w_ref[...], (1, 0))

    pl.semaphore_wait(barrier, group - 1)

    def q_copy(step, slot):
        return pltpu.make_async_remote_copy(
            src_ref=qall_ref.at[slot], dst_ref=qall_ref.at[slot], send_sem=q_send.at[step], recv_sem=q_recv.at[slot],
            device_id=peer(step)[1], device_id_type=MESH)

    def s_copy(step, slot):
        return pltpu.make_async_remote_copy(
            src_ref=sall_ref.at[slot], dst_ref=sall_ref.at[slot], send_sem=s_send.at[step], recv_sem=s_recv.at[slot],
            device_id=peer(step)[1], device_id_type=MESH)

    for step in range(1, group):
        q_copy(step, me).start()
    small[3].wait()

    def doc_part(doc):
        m = jnp.max(best_ref[doc], axis=1, keepdims=True)
        m = jnp.broadcast_to(m, (n_rows * q_len, 128)).reshape(n_rows, q_len, 128)
        return jnp.sum(m, axis=1)

    ones_col = jnp.where(lax.broadcasted_iota(jnp.int32, (n_rows * q_len, 128), 1) == 0, 1.0, 0.0).astype(jnp.bfloat16)
    top_row = lax.broadcasted_iota(jnp.int32, (16, STEP), 0) == 0

    def project(step):
        if step * STEP % CHUNK == 0:
            h_copy(step * STEP // CHUNK).wait()
        h = h_ref[step * STEP:(step + 1) * STEP, :]
        y = lax.dot_general(wt_ref[...], h, (((1,), (1,)), ((), ())), preferred_element_type=jnp.float32)
        inv = lax.rsqrt(jnp.sum(y * y, axis=0, keepdims=True) + NORM_EPS)
        et_ref[step, :proj, :] = (y * inv).astype(jnp.bfloat16)
        doc = step * STEP // d_len
        col = step * STEP % d_len
        valid = dm_ref[doc:doc + 1, col:col + STEP] > 0
        bias = jnp.where(top_row, jnp.where(valid, 0.0, MASKED), 0.0)
        et_ref[step, proj:, :] = bias.astype(jnp.bfloat16)

    def score(step):
        doc = step // doc_steps
        q = qall_ref[...].reshape(n_rows * q_len, proj)
        lhs = jnp.concatenate([q, ones_col], axis=1)
        rhs = jnp.concatenate([et_ref[step], jnp.zeros((TILE - proj - 16, STEP), jnp.bfloat16)], axis=0)
        s = jnp.dot(lhs, rhs, preferred_element_type=jnp.float32)
        m = jnp.maximum(jnp.maximum(s[:, :128], s[:, 128:256]), jnp.maximum(s[:, 256:384], s[:, 384:]))
        if step % doc_steps:
            m = jnp.maximum(m, best_ref[doc])
        best_ref[doc] = m

    for step in range(n_steps + LAG):
        if step == LAG:
            for peer_step in range(1, group):
                q_copy(peer_step, lax.rem(me + peer_step, group)).wait_recv()
        if step < n_steps:
            project(step)
        if step >= LAG:
            score(step - LAG)
        if step == LAG + doc_steps:
            part_ref[0] = doc_part(0)

    lane = lax.broadcasted_iota(jnp.int32, (n_rows, 128), 1)
    first = jnp.where(lane == me * per_dev, part_ref[0], 0.0)
    sall_ref[me] = jnp.where(lane == me * per_dev + 1, doc_part(1), first)

    for step in range(1, group):
        s_copy(step, me).start()
    small[4].wait()
    for step in range(1, group):
        q_copy(step, me).wait_send()
    for step in range(1, group):
        s_copy(step, lax.rem(me + step, group)).wait_recv()

    total = sall_ref[0]
    for d in range(1, group):
        total = total + sall_ref[d]
    logits = total / temp_ref[0]
    logits = jnp.where(lane < n_rows, logits, float('-inf'))
    top = jnp.max(logits, axis=1, keepdims=True)
    log_norm = top + jnp.log(jnp.sum(jnp.exp(logits - top), axis=1, keepdims=True))
    row = lax.broadcasted_iota(jnp.int32, (n_rows, 128), 0)
    own = jnp.sum(jnp.where(row == lane, logits, 0.0), axis=1, keepdims=True)
    loss = jnp.broadcast_to(log_norm - own, (n_rows, 128))
    mean_ref[...] = jnp.sum(loss, axis=0, keepdims=True)[:, :1] / n_rows
    picked = jnp.sum(jnp.where(row == lane + me * per_dev, loss, 0.0), axis=0, keepdims=True)
    rows_ref[...] = picked[:, :per_dev]
    for step in range(1, group):
        s_copy(step, me).wait_send()


def solution(mesh):
    outer = mesh.shape['data2']
    inner = mesh.shape['data']
    group = outer * inner

    def device_fn(q_hidden, d_hidden, w_proj, q_mask, d_mask, value_a11):
        per_dev, q_len, hidden = q_hidden.shape
        d_len = d_hidden.shape[1]
        proj = w_proj.shape[1]
        sizes = (outer, inner, per_dev, q_len, d_len, hidden, proj)
        n_tok = per_dev * d_len
        n_rows = group * per_dev
        any_spec = pl.BlockSpec(memory_space=pl.ANY)
        vmem_spec = pl.BlockSpec(memory_space=pltpu.VMEM)
        rows, mean = pl.pallas_call(
            functools.partial(kernel, sizes),
            out_shape=(jax.ShapeDtypeStruct((1, per_dev), jnp.float32), jax.ShapeDtypeStruct((1, 1), jnp.float32)),
            in_specs=[any_spec] * 6,
            out_specs=(vmem_spec, vmem_spec),
            scratch_shapes=[
                pltpu.VMEM((n_tok, hidden), jnp.bfloat16),
                pltpu.VMEM((per_dev * q_len, hidden), jnp.bfloat16),
                pltpu.VMEM((hidden, proj), jnp.bfloat16),
                pltpu.VMEM((proj, hidden), jnp.bfloat16),
                pltpu.VMEM((per_dev, q_len), jnp.int32),
                pltpu.VMEM((per_dev, d_len), jnp.int32),
                pltpu.SMEM((1,), jnp.float32),
                pltpu.VMEM((n_tok // STEP, proj + 16, STEP), jnp.bfloat16),
                pltpu.VMEM((group, per_dev * q_len, proj), jnp.bfloat16),
                pltpu.VMEM((per_dev, n_rows * q_len, 128), jnp.float32),
                pltpu.VMEM((1, n_rows, 128), jnp.float32),
                pltpu.VMEM((group, n_rows, 128), jnp.float32),
                pltpu.SemaphoreType.DMA((5,)),
                pltpu.SemaphoreType.DMA((n_tok // CHUNK,)),
                pltpu.SemaphoreType.DMA((group,)),
                pltpu.SemaphoreType.DMA((group,)),
                pltpu.SemaphoreType.DMA((group,)),
                pltpu.SemaphoreType.DMA((group,)),
            ],
            compiler_params=pltpu.CompilerParams(
                collective_id=0, has_side_effects=True, vmem_limit_bytes=60 * 1024 * 1024),
            name='colbert_loss',
        )(q_hidden.reshape(per_dev * q_len, hidden), d_hidden.reshape(n_tok, hidden), w_proj, q_mask, d_mask,
          value_a11.reshape(1))
        return rows.reshape(per_dev), mean.reshape(1)

    return jax.shard_map(
        device_fn,
        mesh=mesh,
        in_specs=(P(ROW_AXES), P(ROW_AXES), P(), P(ROW_AXES), P(ROW_AXES), P()),
        out_specs=(P(ROW_AXES), P('replica')),
        check_vma=False,
    )
```

time: 38.3 us -> 27.8 us (0.73)
  Pallas kernels: 33.9 us -> 23.5 us
    pallas_call x1, Pallas kernels: 33.9 us -> 23.5 us  [device_fn(): pl.pallas_call(functools.partial(kernel, sizes), out_shape=(jax.ShapeDtyp...]
where the time goes in v2:
time: 27.8 us; the launch traced here: 27.7 us
  Pallas kernels  23.5 us (85%)
  between operations  3.05 us (11%)
  local copies, waits for them, and re-layouts  1.11 us (4%)
    pallas_call x1, Pallas kernels, device_fn(): pl.pallas_call(functools.partial(kernel, sizes), out_shape=(jax.ShapeDtyp...  23.5 us
    unnamed x1, local copies, waits for them, and re-layouts  1.11 us

profile of v2, /device:TPU:0, one launch (start us, length us, event | category | flops | bytes accessed | tf_op | source)
XLA Modules:
  0.0 27.7 jit_solution(1031375778268275287)
XLA Ops:
  1.3 23.5 %colbert_loss.1 = (f32[1,2]{1,0:T(1,128)}, f32[1,1]{1,0:T(1,128)}) custom-call(bf16[64,768]{1,0:T(8,128)(2,1)} %bitcast.7, bf16[16384,768]{1,0:T(8,128)(2,1)} %bitcast.6, bf16[768,128]{1,0:T(8,128)(2,1)} %w_hbm.1, s32[2,32]{1,0:T(2,128)} %qm_hbm.1, s32[2,8192]{1,0:T(2,128)} %dm_hbm.1, f32[1]{0:T(128)} %bitcast.5.temp_hbm), custom_call_target="tpu_custom_call" | custom-call | tf_op jit(solution)/shard_map/colbert_loss/pallas_call | solution.py:176
  24.8 1.1 %copy.11 = f32[2]{0:T(128)} copy(f32[2]{0:T(128)} %bitcast.8) | data formatting | bytes 16

commit v3 on v2

v3 whole, which is shorter than its diff:
```python
import functools

import jax
import jax.numpy as jnp
from jax import lax
from jax.experimental import pallas as pl
from jax.experimental.pallas import tpu as pltpu
from jax.sharding import PartitionSpec as P

NORM_EPS = 1e-6
ROW_AXES = ('replica', 'data2', 'data')
TILE = 256
STEP = 2 * TILE
CHUNKS = (2, 2, 4, 4, 4, 6, 10)
LAG = 12
PIECE = 256
MASKED = -1e30
MESH = pl.DeviceIdType.MESH


def kernel(sizes, q_hbm, d_hbm, w_hbm, qm_hbm, dm_hbm, out_ref,
           h_ref, q_ref, w_ref, wt_ref, qm_ref, dm_ref, et_ref, qall_ref, best_ref, sall_ref,
           in_sem, h_sem, q_send, q_recv, s_send, s_recv):
    outer, inner, per_dev, q_len, d_len, hidden, proj = sizes
    group = outer * inner
    n_rows = group * per_dev
    n_tok = per_dev * d_len
    starts = [sum(CHUNKS[:i]) for i in range(len(CHUNKS))]
    n_steps = n_tok // STEP
    doc_steps = d_len // STEP
    k_tiles = hidden // TILE
    pieces = n_rows * q_len // PIECE
    q_rows = per_dev * q_len
    d2 = lax.axis_index('data2')
    d1 = lax.axis_index('data')
    me = d2 * inner + d1

    def peer(step):
        other = lax.rem(me + step, group)
        return other, {'data2': other // inner, 'data': lax.rem(other, inner)}

    small = [pltpu.make_async_copy(src, dst, in_sem.at[i]) for i, (src, dst) in enumerate((
        (w_hbm, w_ref), (q_hbm, q_ref), (qm_hbm, qm_ref), (dm_hbm, dm_ref)))]
    for copy in small:
        copy.start()

    barrier = pltpu.get_barrier_semaphore()
    for step in range(1, group):
        pl.semaphore_signal(barrier, inc=1, device_id=peer(step)[1], device_id_type=MESH)

    def h_copy(chunk):
        rows = pl.ds(starts[chunk] * STEP, CHUNKS[chunk] * STEP)
        return pltpu.make_async_copy(d_hbm.at[rows], h_ref.at[rows], h_sem.at[chunk])

    for chunk in range(len(CHUNKS)):
        h_copy(chunk).start(priority=1)

    for copy in small[:3]:
        copy.wait()

    def project_queries():
        y = jnp.dot(q_ref[...], w_ref[...], preferred_element_type=jnp.float32)
        unit = y * lax.rsqrt(jnp.sum(y * y, axis=1, keepdims=True) + NORM_EPS)
        eye = (lax.broadcasted_iota(jnp.int32, (q_len, q_len), 0)
               == lax.broadcasted_iota(jnp.int32, (q_len, q_len), 1))
        for i in range(per_dev):
            keep = jnp.sum(jnp.where(eye, qm_ref[i:i + 1, :], 0), axis=1, keepdims=True)
            rows = jnp.where(keep > 0, unit[i * q_len:(i + 1) * q_len], 0.0)
            qall_ref[me, pl.ds(i * q_len, q_len), :] = rows.astype(jnp.bfloat16)

    project_queries()

    pl.semaphore_wait(barrier, group - 1)

    def q_copy(step, slot):
        return pltpu.make_async_remote_copy(
            src_ref=qall_ref.at[slot], dst_ref=qall_ref.at[slot], send_sem=q_send.at[step], recv_sem=q_recv.at[slot],
            device_id=peer(step)[1], device_id_type=MESH)

    def s_copy(step, slot):
        return pltpu.make_async_remote_copy(
            src_ref=sall_ref.at[slot], dst_ref=sall_ref.at[slot], send_sem=s_send.at[step], recv_sem=s_recv.at[slot],
            device_id=peer(step)[1], device_id_type=MESH)

    for step in range(1, group):
        q_copy(step, me).start()
    wt_ref[...] = jnp.transpose(w_ref[...], (1, 0))
    small[3].wait()

    def doc_row(doc):
        m = jnp.max(best_ref[doc], axis=1, keepdims=True)
        lane = lax.broadcasted_iota(jnp.int32, (n_rows * q_len, 128), 1)
        query = lax.broadcasted_iota(jnp.int32, (n_rows * q_len, 128), 0) // q_len
        return jnp.sum(jnp.where(lane == query, m, 0.0), axis=0, keepdims=True)

    ones_col = jnp.where(lax.broadcasted_iota(jnp.int32, (PIECE, 128), 1) == 0, 1.0, 0.0).astype(jnp.bfloat16)
    top_row = lax.broadcasted_iota(jnp.int32, (16, STEP), 0) == 0
    zeros = jnp.zeros((TILE - proj - 16, STEP), jnp.bfloat16)
    partial = {}

    def project(step, k):
        if k == 0 and step in starts and (step < LAG or step > LAG):
            h_copy(starts.index(step)).wait()
        h = h_ref[step * STEP:(step + 1) * STEP, k * TILE:(k + 1) * TILE]
        y = lax.dot_general(wt_ref[:, k * TILE:(k + 1) * TILE], h, (((1,), (1,)), ((), ())),
                            preferred_element_type=jnp.float32)
        if k:
            y = partial[step] + y
        partial[step] = y
        if k < k_tiles - 1:
            return
        del partial[step]
        inv = lax.rsqrt(jnp.sum(y * y, axis=0, keepdims=True) + NORM_EPS)
        et_ref[step, :proj, :] = (y * inv).astype(jnp.bfloat16)
        doc = step * STEP // d_len
        col = step * STEP % d_len
        valid = dm_ref[doc:doc + 1, col:col + STEP] > 0
        bias = jnp.where(top_row, jnp.where(valid, 0.0, MASKED), 0.0)
        et_ref[step, proj:, :] = bias.astype(jnp.bfloat16)

    def score(step, piece):
        doc = step // doc_steps
        per_piece = PIECE // q_rows
        q = qall_ref[piece * per_piece:(piece + 1) * per_piece].reshape(PIECE, proj)
        lhs = jnp.concatenate([q, ones_col], axis=1)
        rhs = jnp.concatenate([et_ref[step], zeros], axis=0)
        s = jnp.dot(lhs, rhs, preferred_element_type=jnp.float32)
        m = jnp.maximum(jnp.maximum(s[:, :128], s[:, 128:256]), jnp.maximum(s[:, 256:384], s[:, 384:]))
        rows = pl.ds(piece * PIECE, PIECE)
        if step % doc_steps:
            m = jnp.maximum(m, best_ref[doc, rows, :])
        best_ref[doc, rows, :] = m
        if step == doc_steps - 1 and piece == pieces - 1:
            sall_ref[me, 0:1, :] = doc_row(0)

    projects = [(step, k) for step in range(n_steps) for k in range(k_tiles)]
    scores = [(step, piece) for step in range(n_steps) for piece in range(pieces)]
    for item in projects[:LAG * k_tiles]:
        project(*item)
    projects = projects[LAG * k_tiles:]
    for peer_step in range(1, group):
        q_copy(peer_step, lax.rem(me + peer_step, group)).wait_recv()
    if LAG in starts:
        h_copy(starts.index(LAG)).wait()
    while scores:
        score(*scores.pop(0))
        if projects:
            project(*projects.pop(0))

    sall_ref[me, 1:2, :] = doc_row(1)
    for step in range(1, group):
        s_copy(step, me).start()
    for step in range(1, group):
        q_copy(step, me).wait_send()
    for step in range(1, group):
        s_copy(step, lax.rem(me + step, group)).wait_recv()
    out_ref[...] = sall_ref[...].reshape(n_rows, 128)
    for step in range(1, group):
        s_copy(step, me).wait_send()


def finish(sizes, temp_ref, scores_ref, rows_ref, mean_ref):
    outer, inner, per_dev = sizes[:3]
    n_rows = outer * inner * per_dev
    me = lax.axis_index('data2') * inner + lax.axis_index('data')
    lane = lax.broadcasted_iota(jnp.int32, (n_rows, 128), 1)
    doc = lax.broadcasted_iota(jnp.int32, (n_rows, 128), 0)
    logits = scores_ref[...] / temp_ref[0]
    top = jnp.max(logits, axis=0, keepdims=True)
    log_norm = top + jnp.log(jnp.sum(jnp.exp(logits - top), axis=0, keepdims=True))
    loss = log_norm - jnp.sum(jnp.where(doc == lane, logits, 0.0), axis=0, keepdims=True)
    loss = jnp.where(lane[:1] < n_rows, loss, 0.0)
    mean_ref[...] = jnp.sum(loss, axis=1, keepdims=True) / n_rows
    picked = jnp.where(lane[:8] == doc[:8] + me * per_dev, loss, 0.0)
    own = jnp.sum(picked, axis=1, keepdims=True)
    spread = jnp.where(lane[:8] == doc[:8], own, 0.0)
    rows_ref[...] = jnp.sum(spread, axis=0, keepdims=True)[:, :per_dev]


def solution(mesh):
    outer = mesh.shape['data2']
    inner = mesh.shape['data']
    group = outer * inner

    def device_fn(q_hidden, d_hidden, w_proj, q_mask, d_mask, value_a11):
        per_dev, q_len, hidden = q_hidden.shape
        d_len = d_hidden.shape[1]
        proj = w_proj.shape[1]
        sizes = (outer, inner, per_dev, q_len, d_len, hidden, proj)
        n_tok = per_dev * d_len
        n_rows = group * per_dev
        hbm_spec = pl.BlockSpec(memory_space=pltpu.HBM)
        vmem_spec = pl.BlockSpec(memory_space=pltpu.VMEM)
        scores = pl.pallas_call(
            functools.partial(kernel, sizes),
            out_shape=jax.ShapeDtypeStruct((n_rows, 128), jnp.float32),
            in_specs=[hbm_spec] * 5,
            out_specs=vmem_spec,
            scratch_shapes=[
                pltpu.VMEM((n_tok, hidden), jnp.bfloat16),
                pltpu.VMEM((per_dev * q_len, hidden), jnp.bfloat16),
                pltpu.VMEM((hidden, proj), jnp.bfloat16),
                pltpu.VMEM((proj, hidden), jnp.bfloat16),
                pltpu.VMEM((per_dev, q_len), jnp.int32),
                pltpu.VMEM((per_dev, d_len), jnp.int32),
                pltpu.VMEM((n_tok // STEP, proj + 16, STEP), jnp.bfloat16),
                pltpu.VMEM((group, per_dev * q_len, proj), jnp.bfloat16),
                pltpu.VMEM((per_dev, n_rows * q_len, 128), jnp.float32),
                pltpu.VMEM((group, per_dev, 128), jnp.float32),
                pltpu.SemaphoreType.DMA((4,)),
                pltpu.SemaphoreType.DMA((len(CHUNKS),)),
                pltpu.SemaphoreType.DMA((group,)),
                pltpu.SemaphoreType.DMA((group,)),
                pltpu.SemaphoreType.DMA((group,)),
                pltpu.SemaphoreType.DMA((group,)),
            ],
            compiler_params=pltpu.CompilerParams(
                collective_id=0, has_side_effects=True, vmem_limit_bytes=60 * 1024 * 1024),
            name='colbert_loss',
        )(q_hidden.reshape(per_dev * q_len, hidden), d_hidden.reshape(n_tok, hidden), w_proj, q_mask, d_mask)
        rows, mean = pl.pallas_call(
            functools.partial(finish, sizes),
            out_shape=(jax.ShapeDtypeStruct((1, per_dev), jnp.float32), jax.ShapeDtypeStruct((1, 1), jnp.float32)),
            in_specs=[pl.BlockSpec(memory_space=pltpu.SMEM), vmem_spec],
            out_specs=(vmem_spec, vmem_spec),
            name='loss_rows',
        )(value_a11.reshape(1), scores)
        return rows.reshape(per_dev), mean.reshape(1)

    return jax.shard_map(
        device_fn,
        mesh=mesh,
        in_specs=(P(ROW_AXES), P(ROW_AXES), P(), P(ROW_AXES), P(ROW_AXES), P()),
        out_specs=(P(ROW_AXES), P('replica')),
        check_vma=False,
    )
```

time: 27.8 us -> 23.3 us (0.84)
  between operations: 3.05 us -> 1.29 us
  Pallas kernels: 23.5 us -> 21.9 us
  local copies, waits for them, and re-layouts: 1.11 us -> 0 us
    pallas_call x1 -> x2, Pallas kernels: 23.5 us -> 21.9 us  [the longest x1 20.6 us: device_fn(): pl.pallas_call(functools.partial(kernel, sizes), out_shape=jax.ShapeDtype...]
    unnamed x1 -> x0, local copies, waits for them, and re-layouts: 1.11 us -> none
where the time goes in v3:
time: 23.3 us; the launch traced here: 23.2 us
  Pallas kernels  21.9 us (94%)
  between operations  1.29 us (6%)
    pallas_call x1, Pallas kernels, device_fn(): pl.pallas_call(functools.partial(kernel, sizes), out_shape=jax.ShapeDtype...  20.6 us
    pallas_call x1, Pallas kernels, device_fn(): pl.pallas_call(functools.partial(finish, sizes), out_shape=(jax.ShapeDtyp...  1.33 us

profile of v3, /device:TPU:0, one launch (start us, length us, event | category | flops | bytes accessed | tf_op | source)
XLA Modules:
  0.0 23.2 jit_solution(12812990006140323565)
XLA Ops:
  1.3 20.6 %colbert_loss.1.scores_ref = f32[16,128]{1,0:T(8,128)} custom-call(bf16[64,768]{1,0:T(8,128)(2,1)} %bitcast.7, bf16[16384,768]{1,0:T(8,128)(2,1)} %bitcast.6, bf16[768,128]{1,0:T(8,128)(2,1)} %w_hbm.1, s32[2,32]{1,0:T(2,128)} %qm_hbm.1, s32[2,8192]{1,0:T(2,128)} %dm_hbm.1), custom_call_target="tpu_custom_call" | custom-call | tf_op jit(solution)/shard_map/colbert_loss/pallas_call | solution.py:194
  21.8 1.3 %loss_rows.1 = (f32[1,2]{1,0:T(1,128)}, f32[1,1]{1,0:T(1,128)}) custom-call(f32[1]{0:T(128)} %bitcast.5.temp_ref, f32[16,128]{1,0:T(8,128)} %colbert_loss.1.scores_ref), custom_call_target="tpu_custom_call" | custom-call | tf_op jit(solution)/shard_map/loss_rows/pallas_call | solution.py:221

commit v4 on v3

v4 whole, which is shorter than its diff:
```python
import functools

import jax
import jax.numpy as jnp
from jax import lax
from jax.experimental import pallas as pl
from jax.experimental.pallas import tpu as pltpu
from jax.sharding import PartitionSpec as P

NORM_EPS = 1e-6
ROW_AXES = ('replica', 'data2', 'data')
TILE = 256
STEP = 2 * TILE
CHUNKS = (2, 3, 4, 4, 6, 8, 5)
LEAD = 9
EARLY = 12
RESERVE = 5
PIECE = 256
MASKED = -1e30
MESH = pl.DeviceIdType.MESH


def kernel(sizes, q_hbm, d_hbm, w_hbm, qm_hbm, dm_hbm, out_ref,
           h_ref, q_ref, w_ref, wt_ref, qm_ref, dm_ref, y_ref, et_ref, qall_ref, best_ref, sall_ref,
           in_sem, h_sem, q_send, q_recv, s_send, s_recv):
    outer, inner, per_dev, q_len, d_len, hidden, proj = sizes
    group = outer * inner
    n_rows = group * per_dev
    n_steps = per_dev * d_len // STEP
    doc_steps = d_len // STEP
    k_tiles = hidden // TILE
    q_rows = per_dev * q_len
    per_piece = PIECE // q_rows
    d2 = lax.axis_index('data2')
    d1 = lax.axis_index('data')
    me = d2 * inner + d1

    def partner(r):
        y = lax.rem(d2 + r // 4, 2)
        x = lax.rem(d1 // 2 + r // 2 % 2, 2)
        core = lax.rem(d1 + r % 2, 2)
        return y, x * 2 + core

    def target(r):
        y, x = partner(r)
        return {'data2': y, 'data': x}

    small = [pltpu.make_async_copy(src, dst, in_sem.at[i]) for i, (src, dst) in enumerate((
        (w_hbm, w_ref), (q_hbm, q_ref), (qm_hbm, qm_ref), (dm_hbm, dm_ref)))]
    for copy in small:
        copy.start()

    barrier = pltpu.get_barrier_semaphore()
    for r in range(1, group):
        pl.semaphore_signal(barrier, inc=1, device_id=target(r), device_id_type=MESH)

    starts = [sum(CHUNKS[:i]) for i in range(len(CHUNKS))]

    def h_copy(chunk):
        rows = pl.ds(starts[chunk] * STEP, CHUNKS[chunk] * STEP)
        return pltpu.make_async_copy(d_hbm.at[rows], h_ref.at[rows], h_sem.at[chunk])

    for chunk in range(len(CHUNKS)):
        h_copy(chunk).start(priority=1)

    for copy in small[:3]:
        copy.wait()
    y = jnp.dot(q_ref[...], w_ref[...], preferred_element_type=jnp.float32)
    unit = y * lax.rsqrt(jnp.sum(y * y, axis=1, keepdims=True) + NORM_EPS)
    eye = (lax.broadcasted_iota(jnp.int32, (q_len, q_len), 0)
           == lax.broadcasted_iota(jnp.int32, (q_len, q_len), 1))
    for i in range(per_dev):
        keep = jnp.sum(jnp.where(eye, qm_ref[i:i + 1, :], 0), axis=1, keepdims=True)
        rows = jnp.where(keep > 0, unit[i * q_len:(i + 1) * q_len], 0.0)
        qall_ref[0, i * q_len:(i + 1) * q_len, :] = rows.astype(jnp.bfloat16)

    pl.semaphore_wait(barrier, group - 1)

    def q_copy(r):
        return pltpu.make_async_remote_copy(
            src_ref=qall_ref.at[0], dst_ref=qall_ref.at[r], send_sem=q_send, recv_sem=q_recv.at[r // per_piece],
            device_id=target(r), device_id_type=MESH)

    def s_copy(r, slot):
        return pltpu.make_async_remote_copy(
            src_ref=sall_ref.at[slot], dst_ref=sall_ref.at[slot], send_sem=s_send, recv_sem=s_recv,
            device_id=target(r), device_id_type=MESH)

    for r in range(1, group):
        q_copy(r).start()
    wt_ref[...] = jnp.transpose(w_ref[...], (1, 0))
    small[3].wait()

    def doc_row(doc):
        lane = lax.broadcasted_iota(jnp.int32, (q_rows, 128), 1)
        query = lax.broadcasted_iota(jnp.int32, (q_rows, 128), 0) // q_len
        total = jnp.zeros((q_rows, 128), jnp.float32)
        for r in range(group):
            m = jnp.max(best_ref[doc, r * q_rows:(r + 1) * q_rows, :], axis=1, keepdims=True)
            py, px = partner(r)
            total = jnp.where(lane - (py * inner + px) * per_dev == query, m, total)
        return jnp.sum(total, axis=0, keepdims=True)

    ones_col = jnp.where(lax.broadcasted_iota(jnp.int32, (PIECE, 128), 1) == 0, 1.0, 0.0).astype(jnp.bfloat16)
    top_row = lax.broadcasted_iota(jnp.int32, (16, STEP), 0) == 0
    zeros = jnp.zeros((TILE - proj - 16, STEP), jnp.bfloat16)

    def project(step, k):
        h = h_ref[step * STEP:(step + 1) * STEP, k * TILE:(k + 1) * TILE]
        y = lax.dot_general(wt_ref[:, k * TILE:(k + 1) * TILE], h, (((1,), (1,)), ((), ())),
                            preferred_element_type=jnp.float32)
        slot = step % 2 + me // group
        if k:
            y = y_ref[slot] + y
        if k < k_tiles - 1:
            y_ref[slot] = y
            return
        inv = lax.rsqrt(jnp.sum(y * y, axis=0, keepdims=True) + NORM_EPS)
        et_ref[step, :proj, :] = (y * inv).astype(jnp.bfloat16)
        doc = step * STEP // d_len
        col = step * STEP % d_len
        valid = dm_ref[doc:doc + 1, col:col + STEP] > 0
        bias = jnp.where(top_row, jnp.where(valid, 0.0, MASKED), 0.0)
        et_ref[step, proj:, :] = bias.astype(jnp.bfloat16)

    def score(step, piece):
        doc = step // doc_steps
        q = qall_ref[piece * per_piece:(piece + 1) * per_piece].reshape(PIECE, proj)
        lhs = jnp.concatenate([q, ones_col], axis=1)
        rhs = jnp.concatenate([et_ref[step], zeros], axis=0)
        s = jnp.dot(lhs, rhs, preferred_element_type=jnp.float32)
        m = jnp.maximum(jnp.maximum(s[:, :128], s[:, 128:256]), jnp.maximum(s[:, 256:384], s[:, 384:]))
        rows = pl.ds(piece * PIECE, PIECE)
        if step % doc_steps:
            m = jnp.maximum(m, best_ref[doc, rows, :])
        best_ref[doc, rows, :] = m
        if step == doc_steps - 1 and piece == 1:
            sall_ref[me, 0:1, :] = doc_row(0)

    def receive(piece):
        landed = qall_ref.at[max(1, piece * per_piece):(piece + 1) * per_piece]
        pltpu.make_async_copy(landed, landed, q_recv.at[piece]).wait()

    projects = [(step, k) for step in range(n_steps) for k in range(k_tiles)]
    scores = ([(step, 0) for step in range(EARLY)] + [(step, 1) for step in range(EARLY)]
              + [(step, piece) for step in range(EARLY, n_steps) for piece in range(2)])

    pending = list(starts)

    def arrive():
        if projects and projects[0][1] == 0 and projects[0][0] in pending:
            pending.remove(projects[0][0])
            h_copy(starts.index(projects[0][0])).wait()

    for _ in range(LEAD * k_tiles):
        arrive()
        project(*projects.pop(0))
    spare = len(projects) - (len(scores) - RESERVE)
    for i, item in enumerate(scores):
        if i in (0, EARLY):
            receive(i // EARLY)
        arrive()
        score(*item)
        for _ in range(2 if i < spare else 1):
            if projects:
                arrive()
                project(*projects.pop(0))

    sall_ref[me, 1:2, :] = doc_row(1)

    for r in range(1, group):
        s_copy(r, me).start()
    others = qall_ref.at[1:]
    pltpu.make_async_copy(others, others, q_send).wait()
    others = sall_ref.at[1:]
    pltpu.make_async_copy(others, others, s_recv).wait()
    out_ref[...] = sall_ref[...].reshape(n_rows, 128)
    pltpu.make_async_copy(others, others, s_send).wait()


def finish(sizes, temp_ref, scores_ref, rows_ref, mean_ref):
    outer, inner, per_dev = sizes[:3]
    n_rows = outer * inner * per_dev
    me = lax.axis_index('data2') * inner + lax.axis_index('data')
    lane = lax.broadcasted_iota(jnp.int32, (n_rows, 128), 1)
    doc = lax.broadcasted_iota(jnp.int32, (n_rows, 128), 0)
    logits = scores_ref[...] / temp_ref[0]
    top = jnp.max(logits, axis=0, keepdims=True)
    log_norm = top + jnp.log(jnp.sum(jnp.exp(logits - top), axis=0, keepdims=True))
    loss = log_norm - jnp.sum(jnp.where(doc == lane, logits, 0.0), axis=0, keepdims=True)
    loss = jnp.where(lane[:1] < n_rows, loss, 0.0)
    mean_ref[...] = jnp.sum(loss, axis=1, keepdims=True) / n_rows
    picked = jnp.where(lane[:8] == doc[:8] + me * per_dev, loss, 0.0)
    own = jnp.sum(picked, axis=1, keepdims=True)
    spread = jnp.where(lane[:8] == doc[:8], own, 0.0)
    rows_ref[...] = jnp.sum(spread, axis=0, keepdims=True)[:, :per_dev]


def solution(mesh):
    outer = mesh.shape['data2']
    inner = mesh.shape['data']
    group = outer * inner

    def device_fn(q_hidden, d_hidden, w_proj, q_mask, d_mask, value_a11):
        per_dev, q_len, hidden = q_hidden.shape
        d_len = d_hidden.shape[1]
        proj = w_proj.shape[1]
        sizes = (outer, inner, per_dev, q_len, d_len, hidden, proj)
        n_tok = per_dev * d_len
        n_rows = group * per_dev
        hbm_spec = pl.BlockSpec(memory_space=pltpu.HBM)
        vmem_spec = pl.BlockSpec(memory_space=pltpu.VMEM)
        scores = pl.pallas_call(
            functools.partial(kernel, sizes),
            out_shape=pltpu.VMEM((n_rows, 128), jnp.float32),
            in_specs=[hbm_spec] * 5,
            out_specs=vmem_spec,
            scratch_shapes=[
                pltpu.VMEM((n_tok, hidden), jnp.bfloat16),
                pltpu.VMEM((per_dev * q_len, hidden), jnp.bfloat16),
                pltpu.VMEM((hidden, proj), jnp.bfloat16),
                pltpu.VMEM((proj, hidden), jnp.bfloat16),
                pltpu.VMEM((per_dev, q_len), jnp.int32),
                pltpu.VMEM((per_dev, d_len), jnp.int32),
                pltpu.VMEM((2, proj, STEP), jnp.float32),
                pltpu.VMEM((n_tok // STEP, proj + 16, STEP), jnp.bfloat16),
                pltpu.VMEM((group, per_dev * q_len, proj), jnp.bfloat16),
                pltpu.VMEM((per_dev, n_rows * q_len, 128), jnp.float32),
                pltpu.VMEM((group, per_dev, 128), jnp.float32),
                pltpu.SemaphoreType.DMA((4,)),
                pltpu.SemaphoreType.DMA((len(CHUNKS),)),
                pltpu.SemaphoreType.DMA(()),
                pltpu.SemaphoreType.DMA((2,)),
                pltpu.SemaphoreType.DMA(()),
                pltpu.SemaphoreType.DMA(()),
            ],
            compiler_params=pltpu.CompilerParams(
                collective_id=0, has_side_effects=True, vmem_limit_bytes=60 * 1024 * 1024),
            name='colbert_scores',
        )(q_hidden.reshape(per_dev * q_len, hidden), d_hidden.reshape(n_tok, hidden), w_proj, q_mask, d_mask)
        rows, mean = pl.pallas_call(
            functools.partial(finish, sizes),
            out_shape=(jax.ShapeDtypeStruct((1, per_dev), jnp.float32), jax.ShapeDtypeStruct((1, 1), jnp.float32)),
            in_specs=[pl.BlockSpec(memory_space=pltpu.SMEM), vmem_spec],
            out_specs=(vmem_spec, vmem_spec),
            name='loss_rows',
        )(value_a11.reshape(1), pltpu.with_memory_space_constraint(scores, pltpu.VMEM))
        return rows.reshape(per_dev), mean.reshape(1)

    return jax.shard_map(
        device_fn,
        mesh=mesh,
        in_specs=(P(ROW_AXES), P(ROW_AXES), P(), P(ROW_AXES), P(ROW_AXES), P()),
        out_specs=(P(ROW_AXES), P('replica')),
        check_vma=False,
    )
```

time: 23.3 us -> 20.9 us (0.90)
  Pallas kernels: 21.9 us -> 19.5 us
    pallas_call x1, Pallas kernels: 20.6 us -> 18.8 us  [device_fn(): pl.pallas_call(functools.partial(kernel, sizes), out_shape=pltpu.VMEM((n_...]
    pallas_call x1, Pallas kernels: 1.33 us -> 0.64 us  [device_fn(): pl.pallas_call(functools.partial(finish, sizes), out_shape=(jax.ShapeDtyp...]
where the time goes in v4:
time: 20.9 us; the launch traced here: 20.7 us
  Pallas kernels  19.5 us (93%)
  between operations  1.29 us (6%)
    pallas_call x1, Pallas kernels, device_fn(): pl.pallas_call(functools.partial(kernel, sizes), out_shape=pltpu.VMEM((n_...  18.8 us
    pallas_call x1, Pallas kernels, device_fn(): pl.pallas_call(functools.partial(finish, sizes), out_shape=(jax.ShapeDtyp...  0.64 us

profile of v4, /device:TPU:0, one launch (start us, length us, event | category | flops | bytes accessed | tf_op | source)
XLA Modules:
  0.0 20.7 jit_solution(4112162092894618098)
XLA Ops:
  1.3 18.8 %colbert_scores.1.scores_ref = f32[16,128]{1,0:T(8,128)S(1)} custom-call(bf16[64,768]{1,0:T(8,128)(2,1)} %bitcast.7, bf16[16384,768]{1,0:T(8,128)(2,1)} %bitcast.6, bf16[768,128]{1,0:T(8,128)(2,1)} %w_hbm.1, s32[2,32]{1,0:T(2,128)} %qm_hbm.1, s32[2,8192]{1,0:T(2,128)} %dm_hbm.1), custom_call_target="tpu_custom_call" | custom-call | tf_op jit(solution)/shard_map/colbert_scores/pallas_call | solution.py:213
  20.1 0.6 %loss_rows.1 = (f32[1,2]{1,0:T(1,128)}, f32[1,1]{1,0:T(1,128)}) custom-call(f32[1]{0:T(128)} %bitcast.5.temp_ref, f32[16,128]{1,0:T(8,128)S(1)} %colbert_scores.1.scores_ref), custom_call_target="tpu_custom_call" | custom-call | tf_op jit(solution)/shard_map/loss_rows/pallas_call | solution.py:241

commit v5 on v4

--- a/solution.py
+++ b/solution.py
@@ -11,17 +11,18 @@
 ROW_AXES = ('replica', 'data2', 'data')
 TILE = 256
 STEP = 2 * TILE
-CHUNKS = (2, 3, 4, 4, 6, 8, 5)
-LEAD = 9
-EARLY = 12
+CHUNKS = (2,3,6,5,7,9)
+LEAD = 5
+EARLY = 9
 RESERVE = 5
+TURN = 1
 PIECE = 256
 MASKED = -1e30
 MESH = pl.DeviceIdType.MESH
 
 
 def kernel(sizes, q_hbm, d_hbm, w_hbm, qm_hbm, dm_hbm, out_ref,
-           h_ref, q_ref, w_ref, wt_ref, qm_ref, dm_ref, y_ref, et_ref, qall_ref, best_ref, sall_ref,
+           h_ref, q_ref, w_ref, wt_ref, qm_ref, dm_ref, y_ref, ht_ref, et_ref, qall_ref, best_ref, sall_ref,
            in_sem, h_sem, q_send, q_recv, s_send, s_recv):
     outer, inner, per_dev, q_len, d_len, hidden, proj = sizes
     group = outer * inner
@@ -47,21 +48,23 @@
 
     small = [pltpu.make_async_copy(src, dst, in_sem.at[i]) for i, (src, dst) in enumerate((
         (w_hbm, w_ref), (q_hbm, q_ref), (qm_hbm, qm_ref), (dm_hbm, dm_ref)))]
-    for copy in small:
-        copy.start()
+    small[0].start()
+    small[1].start()
+
+    starts = [sum(CHUNKS[:i]) for i in range(len(CHUNKS))]
+
+    def h_copy(chunk):
+        rows = pl.ds(starts[chunk] * STEP, CHUNKS[chunk] * STEP)
+        return pltpu.make_async_copy(d_hbm.at[rows], h_ref.at[rows], h_sem.at[chunk])
+
+    for chunk in range(len(CHUNKS)):
+        h_copy(chunk).start(priority=1)
+    small[2].start()
+    small[3].start()
 
     barrier = pltpu.get_barrier_semaphore()
     for r in range(1, group):
         pl.semaphore_signal(barrier, inc=1, device_id=target(r), device_id_type=MESH)
-
-    starts = [sum(CHUNKS[:i]) for i in range(len(CHUNKS))]
-
-    def h_copy(chunk):
-        rows = pl.ds(starts[chunk] * STEP, CHUNKS[chunk] * STEP)
-        return pltpu.make_async_copy(d_hbm.at[rows], h_ref.at[rows], h_sem.at[chunk])
-
-    for chunk in range(len(CHUNKS)):
-        h_copy(chunk).start(priority=1)
 
     for copy in small[:3]:
         copy.wait()
@@ -105,10 +108,20 @@
     top_row = lax.broadcasted_iota(jnp.int32, (16, STEP), 0) == 0
     zeros = jnp.zeros((TILE - proj - 16, STEP), jnp.bfloat16)
 
+    turned = []
+
+    def turn_tile(step, k):
+        slot = len(turned) % 2 + me // group
+        turned.append((step, k, slot))
+        ht_ref[slot] = jnp.transpose(h_ref[step * STEP:(step + 1) * STEP, k * TILE:(k + 1) * TILE], (1, 0))
+
     def project(step, k):
         h = h_ref[step * STEP:(step + 1) * STEP, k * TILE:(k + 1) * TILE]
-        y = lax.dot_general(wt_ref[:, k * TILE:(k + 1) * TILE], h, (((1,), (1,)), ((), ())),
-                            preferred_element_type=jnp.float32)
+        w = wt_ref[:, k * TILE:(k + 1) * TILE]
+        if turned and turned[-1][:2] == (step, k):
+            y = jnp.dot(w, ht_ref[turned[-1][2]], preferred_element_type=jnp.float32)
+        else:
+            y = lax.dot_general(w, h, (((1,), (1,)), ((), ())), preferred_element_type=jnp.float32)
         slot = step % 2 + me // group
         if k:
             y = y_ref[slot] + y
@@ -147,23 +160,32 @@
 
     pending = list(starts)
 
-    def arrive():
-        if projects and projects[0][1] == 0 and projects[0][0] in pending:
-            pending.remove(projects[0][0])
-            h_copy(starts.index(projects[0][0])).wait()
-
-    for _ in range(LEAD * k_tiles):
-        arrive()
-        project(*projects.pop(0))
+    def arrive(count=1):
+        for item in projects[:count]:
+            if item[1] == 0 and item[0] in pending:
+                pending.remove(item[0])
+                h_copy(starts.index(item[0])).wait()
+
+    lead = LEAD * k_tiles
+    while lead > 0:
+        pair = min(2, lead)
+        arrive(pair)
+        if pair == 2 and TURN:
+            turn_tile(*projects[1])
+        for _ in range(pair):
+            project(*projects.pop(0))
+        lead -= pair
     spare = len(projects) - (len(scores) - RESERVE)
     for i, item in enumerate(scores):
+        count = 2 if i < spare else 1
         if i in (0, EARLY):
             receive(i // EARLY)
-        arrive()
+        arrive(count)
+        if count == 2 and len(projects) > 1:
+            turn_tile(*projects[1])
         score(*item)
-        for _ in range(2 if i < spare else 1):
+        for _ in range(count):
             if projects:
-                arrive()
                 project(*projects.pop(0))
 
     sall_ref[me, 1:2, :] = doc_row(1)
@@ -223,6 +245,7 @@
                 pltpu.VMEM((per_dev, q_len), jnp.int32),
                 pltpu.VMEM((per_dev, d_len), jnp.int32),
                 pltpu.VMEM((2, proj, STEP), jnp.float32),
+                pltpu.VMEM((2, TILE, STEP), jnp.bfloat16),
                 pltpu.VMEM((n_tok // STEP, proj + 16, STEP), jnp.bfloat16),
                 pltpu.VMEM((group, per_dev * q_len, proj), jnp.bfloat16),
                 pltpu.VMEM((per_dev, n_rows * q_len, 128), jnp.float32),

time: 20.9 us -> 19.9 us (0.952)
  Pallas kernels: 19.5 us -> 18.6 us
    pallas_call x1, Pallas kernels: 18.8 us -> 17.9 us  [device_fn(): pl.pallas_call(functools.partial(kernel, sizes), out_shape=pltpu.VMEM((n_...]
where the time goes in v5:
time: 19.9 us; the launch traced here: 19.8 us
  Pallas kernels  18.6 us (93%)
  between operations  1.29 us (6%)
    pallas_call x1, Pallas kernels, device_fn(): pl.pallas_call(functools.partial(kernel, sizes), out_shape=pltpu.VMEM((n_...  17.9 us
    pallas_call x1, Pallas kernels, device_fn(): pl.pallas_call(functools.partial(finish, sizes), out_shape=(jax.ShapeDtyp...  0.64 us

profile of v5, /device:TPU:0, one launch (start us, length us, event | category | flops | bytes accessed | tf_op | source)
XLA Modules:
  0.0 19.8 jit_solution(11880281173741052898)
XLA Ops:
  1.3 17.9 %colbert_scores.1.scores_ref = f32[16,128]{1,0:T(8,128)S(1)} custom-call(bf16[64,768]{1,0:T(8,128)(2,1)} %bitcast.7, bf16[16384,768]{1,0:T(8,128)(2,1)} %bitcast.6, bf16[768,128]{1,0:T(8,128)(2,1)} %w_hbm.1, s32[2,32]{1,0:T(2,128)} %qm_hbm.1, s32[2,8192]{1,0:T(2,128)} %dm_hbm.1), custom_call_target="tpu_custom_call" | custom-call | tf_op jit(solution)/shard_map/colbert_scores/pallas_call | solution.py:235
  19.2 0.6 %loss_rows.1 = (f32[1,2]{1,0:T(1,128)}, f32[1,1]{1,0:T(1,128)}) custom-call(f32[1]{0:T(128)} %bitcast.5.temp_ref, f32[16,128]{1,0:T(8,128)S(1)} %colbert_scores.1.scores_ref), custom_call_target="tpu_custom_call" | custom-call | tf_op jit(solution)/shard_map/loss_rows/pallas_call | solution.py:264

commit v6 on v5

--- a/solution.py
+++ b/solution.py
@@ -11,7 +11,7 @@
 ROW_AXES = ('replica', 'data2', 'data')
 TILE = 256
 STEP = 2 * TILE
-CHUNKS = (2,3,6,5,7,9)
+CHUNKS = (2, 3, 6, 5, 7, 9)
 LEAD = 5
 EARLY = 9
 RESERVE = 5
@@ -42,6 +42,18 @@
         core = lax.rem(d1 + r % 2, 2)
         return y, x * 2 + core
 
+    def place(r):
+        x = partner(r)[1] // 2
+        across, along = r // 2 % 2, r // 4
+        return r % 2 + x * (2 * along + 4 * across) + (1 - x) * (2 * across + 4 * along)
+
+    def holder(slot):
+        first, second = slot // 2 % 2, slot // 4
+        side = d1 // 2
+        y = lax.rem(d2 + side * first + (1 - side) * second, 2)
+        x = lax.rem(side + side * second + (1 - side) * first, 2)
+        return y * inner + x * 2 + lax.rem(d1 + slot % 2, 2)
+
     def target(r):
         y, x = partner(r)
         return {'data2': y, 'data': x}
@@ -81,7 +93,8 @@
 
     def q_copy(r):
         return pltpu.make_async_remote_copy(
-            src_ref=qall_ref.at[0], dst_ref=qall_ref.at[r], send_sem=q_send, recv_sem=q_recv.at[r // per_piece],
+            src_ref=qall_ref.at[0], dst_ref=qall_ref.at[place(r)], send_sem=q_send,
+            recv_sem=q_recv.at[place(r) // per_piece],
             device_id=target(r), device_id_type=MESH)
 
     def s_copy(r, slot):
@@ -100,8 +113,7 @@
         total = jnp.zeros((q_rows, 128), jnp.float32)
         for r in range(group):
             m = jnp.max(best_ref[doc, r * q_rows:(r + 1) * q_rows, :], axis=1, keepdims=True)
-            py, px = partner(r)
-            total = jnp.where(lane - (py * inner + px) * per_dev == query, m, total)
+            total = jnp.where(lane - holder(r) * per_dev == query, m, total)
         return jnp.sum(total, axis=0, keepdims=True)
 
     ones_col = jnp.where(lax.broadcasted_iota(jnp.int32, (PIECE, 128), 1) == 0, 1.0, 0.0).astype(jnp.bfloat16)

time: 19.9 us -> 19.9 us (level)
  no operation moved by 1% of the time
where the time goes in v6:
time: 19.9 us; the launch traced here: 19.8 us
  Pallas kernels  18.5 us (93%)
  between operations  1.29 us (6%)
    pallas_call x1, Pallas kernels, device_fn(): pl.pallas_call(functools.partial(kernel, sizes), out_shape=pltpu.VMEM((n_...  17.9 us
    pallas_call x1, Pallas kernels, device_fn(): pl.pallas_call(functools.partial(finish, sizes), out_shape=(jax.ShapeDtyp...  0.64 us

profile of v6, /device:TPU:0, one launch (start us, length us, event | category | flops | bytes accessed | tf_op | source)
XLA Modules:
  0.0 19.8 jit_solution(2622697590215203198)
XLA Ops:
  1.3 17.9 %colbert_scores.1.scores_ref = f32[16,128]{1,0:T(8,128)S(1)} custom-call(bf16[64,768]{1,0:T(8,128)(2,1)} %bitcast.7, bf16[16384,768]{1,0:T(8,128)(2,1)} %bitcast.6, bf16[768,128]{1,0:T(8,128)(2,1)} %w_hbm.1, s32[2,32]{1,0:T(2,128)} %qm_hbm.1, s32[2,8192]{1,0:T(2,128)} %dm_hbm.1), custom_call_target="tpu_custom_call" | custom-call | tf_op jit(solution)/shard_map/colbert_scores/pallas_call | solution.py:247
  19.2 0.6 %loss_rows.1 = (f32[1,2]{1,0:T(1,128)}, f32[1,1]{1,0:T(1,128)}) custom-call(f32[1]{0:T(128)} %bitcast.5.temp_ref, f32[16,128]{1,0:T(8,128)S(1)} %colbert_scores.1.scores_ref), custom_call_target="tpu_custom_call" | custom-call | tf_op jit(solution)/shard_map/loss_rows/pallas_call | solution.py:276

commit v7 on v6

--- a/solution.py
+++ b/solution.py
@@ -78,7 +78,7 @@
     for r in range(1, group):
         pl.semaphore_signal(barrier, inc=1, device_id=target(r), device_id_type=MESH)
 
-    for copy in small[:3]:
+    for copy in small:
         copy.wait()
     y = jnp.dot(q_ref[...], w_ref[...], preferred_element_type=jnp.float32)
     unit = y * lax.rsqrt(jnp.sum(y * y, axis=1, keepdims=True) + NORM_EPS)
@@ -89,6 +89,7 @@
         rows = jnp.where(keep > 0, unit[i * q_len:(i + 1) * q_len], 0.0)
         qall_ref[0, i * q_len:(i + 1) * q_len, :] = rows.astype(jnp.bfloat16)
 
+    wt_ref[...] = jnp.transpose(w_ref[...], (1, 0))
     pl.semaphore_wait(barrier, group - 1)
 
     def q_copy(r):
@@ -102,10 +103,8 @@
             src_ref=sall_ref.at[slot], dst_ref=sall_ref.at[slot], send_sem=s_send, recv_sem=s_recv,
             device_id=target(r), device_id_type=MESH)
 
-    for r in range(1, group):
+    for r in (4, 2, 5, 3, 6, 7, 1):
         q_copy(r).start()
-    wt_ref[...] = jnp.transpose(w_ref[...], (1, 0))
-    small[3].wait()
 
     def doc_row(doc):
         lane = lax.broadcasted_iota(jnp.int32, (q_rows, 128), 1)

time: 19.9 us -> 19.9 us (level)
  no operation moved by 1% of the time
where the time goes in v7:
time: 19.9 us; the launch traced here: 19.8 us
  Pallas kernels  18.5 us (93%)
  between operations  1.29 us (6%)
    pallas_call x1, Pallas kernels, device_fn(): pl.pallas_call(functools.partial(kernel, sizes), out_shape=pltpu.VMEM((n_...  17.9 us
    pallas_call x1, Pallas kernels, device_fn(): pl.pallas_call(functools.partial(finish, sizes), out_shape=(jax.ShapeDtyp...  0.64 us

profile of v7, /device:TPU:0, one launch (start us, length us, event | category | flops | bytes accessed | tf_op | source)
XLA Modules:
  0.0 19.8 jit_solution(17475332044193752738)
XLA Ops:
  1.3 17.9 %colbert_scores.1.scores_ref = f32[16,128]{1,0:T(8,128)S(1)} custom-call(bf16[64,768]{1,0:T(8,128)(2,1)} %bitcast.7, bf16[16384,768]{1,0:T(8,128)(2,1)} %bitcast.6, bf16[768,128]{1,0:T(8,128)(2,1)} %w_hbm.1, s32[2,32]{1,0:T(2,128)} %qm_hbm.1, s32[2,8192]{1,0:T(2,128)} %dm_hbm.1), custom_call_target="tpu_custom_call" | custom-call | tf_op jit(solution)/shard_map/colbert_scores/pallas_call | solution.py:246
  19.2 0.6 %loss_rows.1 = (f32[1,2]{1,0:T(1,128)}, f32[1,1]{1,0:T(1,128)}) custom-call(f32[1]{0:T(128)} %bitcast.5.temp_ref, f32[16,128]{1,0:T(8,128)S(1)} %colbert_scores.1.scores_ref), custom_call_target="tpu_custom_call" | custom-call | tf_op jit(solution)/shard_map/loss_rows/pallas_call | solution.py:275
